TPU v7x, 32 devices: a whole 2x2x4 slice. The times are simulated.
32 devices in a mesh: row: 8 (over z, x), col: 4 (over y, core).
Axes of the slice: x: 2, y: 2, z: 4, core: 2. Of those that a mesh axis runs over, the one named last changes fastest.
Arguments:
- features: bfloat16 [4096, 512], P(('row', 'col')), may hold values from -6 to 6
- adjacency: bfloat16 [4096, 4096], P('row', 'col'), may hold values from -0.546875 to 0.546875
- block_pattern: int32 [64, 64], P('row', 'col'), may hold values from 0 to 1, as said below
- weight_in: bfloat16 [512, 256], replicated, may hold values from -0.25 to 0.25
- bias_in: float32 [256], replicated, may hold values from -3 to 3
- weight_out: bfloat16 [256, 256], replicated, may hold values from -0.75 to 0.75
- bias_out: float32 [256], replicated, may hold values from -3 to 3
Outputs:
- embeddings: bfloat16 [4096, 256], P(('row', 'col'))
Inputs may be any that keep to these rules, and one draw needn't show every extreme that they name: `block_pattern`: in each aligned tile of 8 rows by 16 columns, at most half of the entries are 1; some tile has exactly half.
All inputs are finite; a program needn't handle non-finite values.
Results may differ from a plain program's by a relative error of at most 0.015.
Values may be sent and summed in bfloat16 or wider, within the bound.
A program may use at most 64 MiB of HBM per device.

v0:
```python
import jax
import jax.numpy as jnp
from jax import lax
from jax.sharding import PartitionSpec as P

BLK = 64


def collect(partial_value):
    return lax.psum_scatter(
        partial_value.astype(jnp.bfloat16), "col", scatter_dimension=0, tiled=True
    ).astype(jnp.float32)


def body(features, adjacency, block_pattern, weight_in, bias_in, weight_out, bias_out):
    row_blocks, col_blocks = block_pattern.shape
    tile_height, tile_width = adjacency.shape
    present = (block_pattern == 1)[:, None, :, None]
    masked = jnp.where(
        present, adjacency.reshape(row_blocks, BLK, col_blocks, BLK), jnp.zeros((), adjacency.dtype)
    )
    masked = masked.reshape(tile_height, tile_width)
    squares = jnp.sum(jnp.square(masked.astype(jnp.float32)), axis=1)

    def product(gathered):
        return jnp.dot(masked, gathered, preferred_element_type=jnp.float32)

    degree = 1.0 + lax.psum_scatter(squares, "col", scatter_dimension=0, tiled=True)
    inv_root = lax.rsqrt(degree)[:, None]
    own_rows = (inv_root * jnp.dot(features, weight_in, preferred_element_type=jnp.float32)).astype(
        jnp.bfloat16
    )
    gathered = lax.all_gather(own_rows, "row", axis=0, tiled=True)
    summed = collect(product(gathered)) + own_rows.astype(jnp.float32)
    hidden = jax.nn.relu(inv_root * summed + bias_in[None, :]).astype(jnp.bfloat16)
    scaled_out = (
        inv_root * jnp.dot(hidden, weight_out, preferred_element_type=jnp.float32)
    ).astype(jnp.bfloat16)
    gathered_out = lax.all_gather(scaled_out, "row", axis=0, tiled=True)
    summed_out = collect(product(gathered_out)) + scaled_out.astype(jnp.float32)
    return (inv_root * summed_out + bias_out[None, :]).astype(jnp.bfloat16)


def solution(mesh):
    placed = (P(("row", "col"), None), P("row", "col"), P("row", "col"), P(), P(), P(), P())
    return jax.shard_map(
        body, mesh=mesh, in_specs=placed, out_specs=P(("row", "col"), None), check_vma=False
    )
```

profile of v0, /device:TPU:0, one launch (start us, length us, event | category | flops | bytes accessed | tf_op | source)
XLA Modules:
  0.0 136.0 jit_solution(15253424916273779903)
XLA Ops:
  6.5 0.7 broadcast_compare_fusion
  7.3 0.3 broadcast_in_dim.18
  7.6 0.0 copy-start.1
  7.6 2.4 %broadcast_in_dim.19 = pred[512,1024]{1,0:T(32,128)(4,1)S(1)} reshape(pred[8,64,16,64]{3,2,1,0:T(8,128)(4,1)S(1)} %broadcast_in_dim.18) | data formatting | bytes 1048576 | tf_op jit(solution)/shard_map/jit(_where)/broadcast_in_dim | solution.py:19
  10.0 0.0 copy-start.6
  10.1 0.0 copy-start.2
  10.1 0.5 multiply_reduce_fusion
  10.6 8.4 %all-reduce = f32[512]{0:T(512)S(1)} all-reduce(f32[512]{0:T(512)S(1)} %multiply_reduce_fusion), channel_id=2, replica_groups=mesh['row'=8,'col'=4] {'col'}, use_global_device_ids=true, to_apply=%region_1.2.clone | all-reduce | flops 512 | bytes 4096
  18.9 0.0 copy-done.6
  18.9 0.6 dynamic-slice
  20.2 0.1 fusion.5
  20.3 0.2 fusion
  20.5 31.9 %all_gather.6 = bf16[1024,256]{1,0:T(8,128)(2,1)S(1)} all-gather(bf16[128,256]{1,0:T(8,128)(2,1)S(1)} %fusion), channel_id=1, replica_groups=mesh['row'=8,'col'=4] {'row'}, dimensions={0}, use_global_device_ids=true | all-gather | bytes 589824 | tf_op jit(solution)/shard_map/all_gather | solution.py:33
  52.4 1.1 convolution_convert_fusion.1
  53.5 0.0 reduce-scatter.3.cloned.1.call-update
  53.5 0.0 reduce-scatter.5.cloned.1.call-start
  53.6 20.0 %reduce-scatter.3.cloned.1.call-done = bf16[128,256]{1,0:T(8,128)(2,1)} async-done(((bf16[512,256]{1,0:T(8,128)(2,1)}), bf16[128,256]{1,0:T(8,128)(2,1)}) %reduce-scatter.3.cloned.1.call-update) | async-done | bytes 65552 | tf_op jit(solution)/shard_map/reduce_scatter | solution.py:10
  73.6 0.0 copy-done.4
  73.6 1.0 fusion.1
  74.7 31.5 %all_gather.7 = bf16[1024,256]{1,0:T(8,128)(2,1)S(1)} all-gather(bf16[128,256]{1,0:T(8,128)(2,1)S(1)} %fusion.1), channel_id=1, replica_groups=mesh['row'=8,'col'=4] {'row'}, dimensions={0}, use_global_device_ids=true | all-gather | bytes 589824 | tf_op jit(solution)/shard_map/all_gather | solution.py:39
  106.1 1.1 convolution_convert_fusion
  107.3 0.0 reduce-scatter.5.cloned.1.call-update
  107.3 20.3 %reduce-scatter.5.cloned.1.call-done = bf16[128,256]{1,0:T(8,128)(2,1)} async-done(((bf16[512,256]{1,0:T(8,128)(2,1)}), bf16[128,256]{1,0:T(8,128)(2,1)}) %reduce-scatter.5.cloned.1.call-update) | async-done | bytes 65552 | tf_op jit(solution)/shard_map/reduce_scatter | solution.py:10
  127.6 1.6 %add_convert_fusion = bf16[128,256]{1,0:T(8,128)(2,1)} fusion(bf16[128,256]{1,0:T(8,128)(2,1)S(1)} %fusion.1, bf16[128,256]{1,0:T(8,128)(2,1)} %reduce-scatter.5.cloned.1.call-done, f32[256]{0:T(256)S(1)} %copy-done.3, f32[128]{0:T(128)S(1)} %fusion.5), kind=kLoop, calls=%fused_computation.8 | loop fusion | flops 196608 | bytes 198144 | tf_op jit(solution)/shard_map/convert_element_type | solution.py:41
  (10 shorter events, 0.0 us)
Async XLA Ops:
  6.5 13.7 %copy-start = (bf16[512,256]{1,0:T(8,128)(2,1)S(1)}, bf16[512,256]{1,0:T(8,128)(2,1)}, u32[]{:S(2)}) copy-start(bf16[512,256]{1,0:T(8,128)(2,1)} %param.10) | copy-start | bytes 786436
  6.5 67.1 %reduce-scatter.3.cloned.1.call-start = ((), (), s32[]{:S(2)}) async-start(), calls=%async_computation.2 | async-start | bytes 327680 | tf_op jit(solution)/shard_map/reduce_scatter | solution.py:10
  7.6 2.4 %copy-start.1 = (bf16[512,1024]{1,0:T(8,128)(2,1)S(1)}, bf16[512,1024]{1,0:T(8,128)(2,1)}, u32[]{:S(2)}) copy-start(bf16[512,1024]{1,0:T(8,128)(2,1)} %param.8) | copy-start | bytes 3145732
  10.0 8.9 %copy-start.6 = (u32[32]{0:T(128)S(1)}, u32[32]{0:T(128)}, u32[]{:S(2)}) copy-start(u32[32]{0:T(128)} %constant.12) | copy-start | bytes 388
  10.1 10.2 %copy-start.2 = (bf16[128,512]{1,0:T(8,128)(2,1)S(1)}, bf16[128,512]{1,0:T(8,128)(2,1)}, u32[]{:S(2)}) copy-start(bf16[128,512]{1,0:T(8,128)(2,1)} %param.7) | copy-start | bytes 393220
  52.3 21.3 %copy-start.4 = (bf16[256,256]{1,0:T(8,128)(2,1)S(1)}, bf16[256,256]{1,0:T(8,128)(2,1)}, u32[]{:S(2)}) copy-start(bf16[256,256]{1,0:T(8,128)(2,1)} %param.12) | copy-start | bytes 393220
  52.4 21.3 %copy-start.5 = (f32[256]{0:T(256)S(1)}, f32[256]{0:T(256)}, u32[]{:S(2)}) copy-start(f32[256]{0:T(256)} %param.11) | copy-start | bytes 3076
  53.5 74.1 %reduce-scatter.5.cloned.1.call-start = ((), (), s32[]{:S(2)}) async-start(), calls=%async_computation.3 | async-start | bytes 327680 | tf_op jit(solution)/shard_map/reduce_scatter | solution.py:10
  106.1 21.5 %copy-start.3 = (f32[256]{0:T(256)S(1)}, f32[256]{0:T(256)}, u32[]{:S(2)}) copy-start(f32[256]{0:T(256)} %param.13) | copy-start | bytes 3076
Sparse Core Ops, SparseCore 0:
  53.6 19.9 reduce-scatter.2
  107.4 20.1 reduce-scatter.4
where the time goes:
time: 136 us
  blocking collectives  71.7 us (53%)
  waiting for transfers between devices  40.4 us (30%)
  between operations  14.1 us (10%)
  matrix products  3.52 us (3%)
  local copies, waits for them, and re-layouts  3.35 us (2%)
  other arithmetic  2.85 us (2%)
    reduce_scatter x2, waiting for transfers between devices, collect(): lax.psum_scatter(partial_value.astype(jnp.bfloat16), 'col', scatter_dimen...  40.4 us
    all_gather x1, blocking collectives, body(): gathered = lax.all_gather(own_rows, 'row', axis=0, tiled=True)  31.9 us
    all_gather x1, blocking collectives, body(): gathered_out = lax.all_gather(scaled_out, 'row', axis=0, tiled=True)  31.5 us
    unnamed x1, blocking collectives  8.4 us
    broadcast_in_dim x2, local copies, waits for them, and re-layouts, body(): jnp.where(present, adjacency.reshape(row_blocks, BLK, col_blocks, BLK), j...  2.73 us
  transfers between devices with their start and end apart: 2, of which 2 were waited for; matrix products, arithmetic and copies ran while one was open for 0% of the time, Pallas kernels for 0%

commit v1 on v0

v1 whole, which is shorter than its diff:
```python
import functools

import jax
import jax.numpy as jnp
from jax import lax
from jax.experimental import pallas as pl
from jax.experimental.pallas import tpu as pltpu
from jax.sharding import PartitionSpec as P

MESH = pl.DeviceIdType.MESH
F32 = jnp.float32
BF16 = jnp.bfloat16
UNROLL = 16


def steps(count, body):
    if count <= UNROLL:
        for step in range(count):
            body(step)
    else:
        pl.loop(0, count)(body)


def kernel(
    n_row, n_col,
    features, adjacency, pattern, weight_in, bias_in, weight_out, bias_out, out,
    masked, squares, total, rows_in, rows_out, scaled, part_in, part_out, got_in, got_out,
    degree_send, degree_got, roots, root_tile,
    send_rows, recv_rows, send_part, recv_part, send_degree, recv_degree, send_root, recv_root,
):
    row, col = lax.axis_index("row"), lax.axis_index("col")
    own, width = rows_in.shape[1], rows_in.shape[2]
    row_blocks = pattern.shape[0]
    side = adjacency.shape[0] // row_blocks

    def row_peer(step):
        return lax.rem(row + step, n_row)

    def col_peer(step):
        return lax.rem(col + step, n_col)

    barrier = pltpu.get_barrier_semaphore()

    def greet_row(step):
        pl.semaphore_signal(barrier, inc=1, device_id=(row_peer(step + 1), col), device_id_type=MESH)

    def greet_col(step):
        pl.semaphore_signal(barrier, inc=1, device_id=(row, col_peer(step + 1)), device_id_type=MESH)

    steps(n_row - 1, greet_row)
    steps(n_col - 1, greet_col)

    def rows_copy(buffer, layer, step):
        return pltpu.make_async_remote_copy(
            src_ref=buffer.at[row], dst_ref=buffer.at[row],
            send_sem=send_rows.at[layer, step], recv_sem=recv_rows.at[layer, step],
            device_id=(row_peer(step), col), device_id_type=MESH,
        )

    def part_copy(source, landing, layer, step):
        return pltpu.make_async_remote_copy(
            src_ref=source.at[col_peer(step)], dst_ref=landing.at[step],
            send_sem=send_part.at[layer, step], recv_sem=recv_part.at[layer, step],
            device_id=(row, col_peer(step)), device_id_type=MESH,
        )

    def degree_copy(step):
        return pltpu.make_async_remote_copy(
            src_ref=degree_send.at[col_peer(step)], dst_ref=degree_got.at[step],
            send_sem=send_degree.at[step], recv_sem=recv_degree.at[step],
            device_id=(row, col_peer(step)), device_id_type=MESH,
        )

    def root_copy(step):
        return pltpu.make_async_remote_copy(
            src_ref=roots.at[row], dst_ref=roots.at[row],
            send_sem=send_root.at[step], recv_sem=recv_root.at[step],
            device_id=(row_peer(step), col), device_id_type=MESH,
        )

    projected = jnp.dot(features[...], weight_in[...], preferred_element_type=F32)
    rows_in[row] = projected.astype(BF16)
    pl.semaphore_wait(barrier, n_row + n_col - 2)
    steps(n_row - 1, lambda step: rows_copy(rows_in, 0, step + 1).start())

    col_blocks = pattern.shape[1]
    lane = lax.broadcasted_iota(jnp.int32, (col_blocks, col_blocks * side), 1)
    block = lax.broadcasted_iota(jnp.int32, (col_blocks, col_blocks * side), 0)
    spread = jnp.where(lane // side == block, 1.0, 0.0).astype(BF16)
    marks = jnp.where(pattern[...] == 1, 1.0, 0.0).astype(BF16)
    wide = jnp.dot(marks, spread, preferred_element_type=F32)
    for owner in range(n_row):
        root_tile[owner] = wide[:, owner * own:(owner + 1) * own]
    squares[...] = jnp.zeros_like(squares)

    def mask_slab(owner):
        start = owner * own if isinstance(owner, int) else pl.multiple_of(owner * own, own)
        for r in range(row_blocks):
            rows = pl.ds(r * side, side)
            mark = root_tile[owner, r:r + 1, :]
            piece = adjacency[rows, pl.ds(start, own)].astype(F32) * mark
            squares[rows, :] += piece * piece
            masked[owner, rows, :] = piece.astype(BF16)

    steps(n_row, mask_slab)
    ones = jnp.ones((8, own), BF16)
    high = squares[...].astype(BF16)
    low = (squares[...] - high.astype(F32)).astype(BF16)
    contract = (((1,), (1,)), ((), ()))
    sums = lax.dot_general(ones, high, contract, preferred_element_type=F32)
    sums = sums + lax.dot_general(ones, low, contract, preferred_element_type=F32)
    for peer in range(n_col):
        degree_send[peer] = sums[:, peer * own:(peer + 1) * own]
    steps(n_col - 1, lambda step: degree_copy(step + 1).start())
    degree_got[0] = degree_send[col]
    for step in range(1, n_col):
        degree_copy(step).wait_recv()
    degree = 1.0 + degree_got[0]
    for step in range(1, n_col):
        degree = degree + degree_got[step]
    roots[row] = lax.rsqrt(degree)
    steps(n_row - 1, lambda step: root_copy(step + 1).start())

    def root_column(owner):
        return jnp.broadcast_to(roots[owner, 0:1, :], (own, own)).T

    def widen(column):
        return jnp.concatenate([column] * (width // own), axis=1)

    inv_root = widen(root_column(row))
    own_in = inv_root * projected

    def layer(buffer, index, first):
        def add(step):
            owner = row_peer(n_row - step)
            if not (isinstance(step, int) and step == 0):
                rows_copy(buffer, index, step).wait_recv()
                if first:
                    root_copy(step).wait_recv()
            values = buffer[owner]
            if first:
                values = (widen(root_column(owner)) * values.astype(F32)).astype(BF16)
            product = jnp.dot(masked[owner], values, preferred_element_type=F32)
            if isinstance(step, int) and step == 0:
                total[...] = product
            else:
                total[...] += product

        add(0)
        if n_row <= UNROLL:
            for step in range(1, n_row):
                add(step)
        else:
            pl.loop(1, n_row)(add)

    def collect(source, landing, index):
        for step in list(range(1, n_col)):
            peer = col_peer(step)
            source[peer] = total[pl.ds(pl.multiple_of(peer * own, own), own), :].astype(BF16)
            part_copy(source, landing, index, step).start()
        mine = total[pl.ds(pl.multiple_of(col * own, own), own), :]
        for step in range(1, n_col):
            part_copy(source, landing, index, step).wait_recv()
            mine = mine + landing[step].astype(F32)
        return mine

    layer(rows_in, 0, True)
    summed = collect(part_in, got_in, 0) + own_in
    hidden = jnp.maximum(inv_root * summed + bias_in[...], 0.0).astype(BF16)
    scaled_out = inv_root * jnp.dot(hidden, weight_out[...], preferred_element_type=F32)
    rows_out[row] = scaled_out.astype(BF16)
    steps(n_row - 1, lambda step: rows_copy(rows_out, 1, step + 1).start())
    layer(rows_out, 1, False)
    summed_out = collect(part_out, got_out, 1) + scaled_out
    out[...] = (inv_root * summed_out + bias_out[...]).astype(BF16)

    def drain_rows(step):
        rows_copy(rows_in, 0, step + 1).wait_send()
        rows_copy(rows_out, 1, step + 1).wait_send()
        root_copy(step + 1).wait_send()

    def drain_cols(step):
        part_copy(part_in, got_in, 0, step + 1).wait_send()
        part_copy(part_out, got_out, 1, step + 1).wait_send()
        degree_copy(step + 1).wait_send()

    steps(n_row - 1, drain_rows)
    steps(n_col - 1, drain_cols)


def body(n_row, n_col, features, adjacency, pattern, weight_in, bias_in, weight_out, bias_out):
    own, width = features.shape[0], weight_out.shape[1]
    height = adjacency.shape[0]
    dma = pltpu.SemaphoreType.DMA
    vmem = pl.BlockSpec(memory_space=pltpu.VMEM)
    return pl.pallas_call(
        functools.partial(kernel, n_row, n_col),
        out_shape=jax.ShapeDtypeStruct((own, width), BF16),
        in_specs=[vmem] * 7,
        out_specs=vmem,
        scratch_shapes=[
            pltpu.VMEM((n_row, height, own), BF16),
            pltpu.VMEM((height, own), F32),
            pltpu.VMEM((height, width), F32),
            pltpu.VMEM((n_row, own, width), BF16),
            pltpu.VMEM((n_row, own, width), BF16),
            pltpu.VMEM((own, width), BF16),
            pltpu.VMEM((n_col, own, width), BF16),
            pltpu.VMEM((n_col, own, width), BF16),
            pltpu.VMEM((n_col, own, width), BF16),
            pltpu.VMEM((n_col, own, width), BF16),
            pltpu.VMEM((n_col, 8, own), F32),
            pltpu.VMEM((n_col, 8, own), F32),
            pltpu.VMEM((n_row, 8, own), F32),
            pltpu.VMEM((n_row, pattern.shape[0], own), F32),
            dma((2, n_row)), dma((2, n_row)), dma((2, n_col)), dma((2, n_col)),
            dma((n_col,)), dma((n_col,)), dma((n_row,)), dma((n_row,)),
        ],
        compiler_params=pltpu.CompilerParams(
            collective_id=0, has_side_effects=True, vmem_limit_bytes=60 * 1024 * 1024
        ),
    )(features, adjacency, pattern, weight_in, bias_in[None, :], weight_out, bias_out[None, :])


def solution(mesh):
    placed = (P(("row", "col"), None), P("row", "col"), P("row", "col"), P(), P(), P(), P())
    return jax.shard_map(
        functools.partial(body, mesh.shape["row"], mesh.shape["col"]),
        mesh=mesh, in_specs=placed, out_specs=P(("row", "col"), None), check_vma=False,
    )
```

time: 136 us -> 44.9 us (0.33)
  the two profiles are of different devices: /device:TPU:0 before, /device:TPU:15 now
where the time goes in v1:
time: 44.9 us; the launch traced here: 44.7 us
  Pallas kernels  43.2 us (96%)
  local copies, waits for them, and re-layouts  1.47 us (3%)
    pallas_call x1, Pallas kernels, body(): pl.pallas_call(functools.partial(kernel, n_row, n_col), out_shape=jax.Sha...  43.2 us
    unnamed x1, local copies, waits for them, and re-layouts  1.47 us

profile of v1, /device:TPU:15, one launch (start us, length us, event | category | flops | bytes accessed | tf_op | source)
XLA Modules:
  0.0 44.7 jit_solution(8883170746186293480)
XLA Ops:
  0.0 43.2 %shard_map.73 = bf16[128,256]{1,0:T(8,128)(2,1)} custom-call(bf16[128,512]{1,0:T(8,128)(2,1)} %features.1, bf16[512,1024]{1,0:T(8,128)(2,1)} %adjacency.1, s32[8,16]{1,0:T(8,128)} %pattern.1, bf16[512,256]{1,0:T(8,128)(2,1)} %weight_in.1, f32[1,256]{1,0:T(1,128)} %bitcast.2, bf16[256,256]{1,0:T(8,128)(2,1)} %weight_out.1, f32[1,256]{1,0:T(1,128)} %bitcast.3), custom_call_target="tpu_custom_call" | custom-call | tf_op jit(solution)/shard_map/pallas_call | solution.py:196
  43.2 1.5 %copy.9 = bf16[128,256]{1,0:T(8,128)(2,1)} copy(bf16[128,256]{1,0:T(8,128)(2,1)} %shard_map.73) | data formatting | bytes 131072

commit v2 on v0

v2 whole, which is shorter than its diff:
```python
import functools

import jax
import jax.numpy as jnp
from jax import lax
from jax.experimental import pallas as pl
from jax.experimental.pallas import tpu as pltpu
from jax.sharding import PartitionSpec as P

MESH = pl.DeviceIdType.MESH
F32 = jnp.float32
BF16 = jnp.bfloat16


def kernel(
    n_lo, n_col,
    features_in, adjacency_in, pattern_in, weight_one_in, bias_one_in, weight_two_in, bias_two_in, out,
    features, adjacency, pattern, weight_in, bias_in, weight_out, bias_out,
    masked, squares, marked, total, rows_in, rows_out, part_in, part_out, got_in, got_out,
    degree_send, degree_got, roots, load,
    send_hi, recv_hi, send_lo, recv_lo, send_part, recv_part,
    send_degree, recv_degree, send_root, recv_root,
):
    row, col = lax.axis_index("row"), lax.axis_index("col")
    halves, n_row, own, width = rows_in.shape
    n_hi = n_row // n_lo
    hi, lo = row // n_lo, row % n_lo
    row_blocks, col_blocks = pattern.shape
    side = adjacency.shape[0] // row_blocks

    def hi_peer(step):
        return lax.rem(hi + step, n_hi) * n_lo + lo

    def lo_peer(step):
        return hi * n_lo + lax.rem(lo + step, n_lo)

    def col_peer(step):
        return lax.rem(col + step, n_col)

    barrier = pltpu.get_barrier_semaphore()

    def greet(target):
        pl.semaphore_signal(barrier, inc=1, device_id=target, device_id_type=MESH)

    for step in range(1, n_hi):
        greet((hi_peer(step), col))
    for step in range(1, n_lo):
        greet((lo_peer(step), col))
    for step in range(1, n_col):
        greet((row, col_peer(step)))

    pairs = [
        (features_in, features), (weight_one_in, weight_in), (pattern_in, pattern),
        (adjacency_in, adjacency), (bias_one_in, bias_in), (weight_two_in, weight_out),
        (bias_two_in, bias_out),
    ]
    loads = [pltpu.make_async_copy(a, b, load.at[i]) for i, (a, b) in enumerate(pairs)]
    for copy in loads:
        copy.start()

    def hi_copy(buffer, layer, half, step, owner):
        return pltpu.make_async_remote_copy(
            src_ref=buffer.at[half, owner], dst_ref=buffer.at[half, owner],
            send_sem=send_hi.at[layer, half, step], recv_sem=recv_hi.at[layer, half, step],
            device_id=(hi_peer(step), col), device_id_type=MESH,
        )

    def lo_copy(buffer, layer, half, back, step, owner):
        return pltpu.make_async_remote_copy(
            src_ref=buffer.at[half, owner], dst_ref=buffer.at[half, owner],
            send_sem=send_lo.at[layer, half, back, step], recv_sem=recv_lo.at[layer, half, back, step],
            device_id=(lo_peer(step), col), device_id_type=MESH,
        )

    def root_hi(step, owner):
        return pltpu.make_async_remote_copy(
            src_ref=roots.at[owner], dst_ref=roots.at[owner],
            send_sem=send_root.at[step, 0], recv_sem=recv_root.at[step, 0],
            device_id=(hi_peer(step), col), device_id_type=MESH,
        )

    def root_lo(back, step, owner):
        return pltpu.make_async_remote_copy(
            src_ref=roots.at[owner], dst_ref=roots.at[owner],
            send_sem=send_root.at[back, step], recv_sem=recv_root.at[back, step],
            device_id=(lo_peer(step), col), device_id_type=MESH,
        )

    def part_copy(source, landing, layer, half, step):
        return pltpu.make_async_remote_copy(
            src_ref=source.at[half, step], dst_ref=landing.at[half, step],
            send_sem=send_part.at[layer, half, step], recv_sem=recv_part.at[layer, half, step],
            device_id=(row, col_peer(step)), device_id_type=MESH,
        )

    def degree_copy(step):
        return pltpu.make_async_remote_copy(
            src_ref=degree_send.at[col_peer(step)], dst_ref=degree_got.at[step],
            send_sem=send_degree.at[step], recv_sem=recv_degree.at[step],
            device_id=(row, col_peer(step)), device_id_type=MESH,
        )

    def holder(back):
        return lax.rem(hi + n_hi - back, n_hi) * n_lo + lo

    def send_own(buffer, layer):
        for half in range(halves):
            for step in range(1, n_hi):
                hi_copy(buffer, layer, half, step, row).start()
            for step in range(1, n_lo):
                lo_copy(buffer, layer, half, 0, step, row).start()

    def pass_on(buffer, layer, half):
        for back in range(1, n_hi):
            hi_copy(buffer, layer, half, back, row).wait_recv()
            for step in range(1, n_lo):
                lo_copy(buffer, layer, half, back, step, holder(back)).start()

    loads[0].wait()
    loads[1].wait()
    projected = jnp.dot(features[...], weight_in[...], preferred_element_type=F32)
    for half in range(halves):
        rows_in[half, row] = projected[:, half * width:(half + 1) * width].astype(BF16)
    loads[2].wait()
    loads[3].wait()

    lane = lax.broadcasted_iota(jnp.int32, (col_blocks, col_blocks * side), 1)
    block = lax.broadcasted_iota(jnp.int32, (col_blocks, col_blocks * side), 0)
    spread = jnp.where(lane // side == block, 1.0, 0.0).astype(BF16)
    marks = jnp.where(pattern[...] == 1, 1.0, 0.0).astype(BF16)
    wide = jnp.dot(marks, spread, preferred_element_type=F32)
    for owner in range(n_row):
        marked[owner] = wide[:, owner * own:(owner + 1) * own]

    def mask_rows(r):
        start = r * side if isinstance(r, int) else pl.multiple_of(r * side, side)
        rows = pl.ds(start, side)
        square = jnp.zeros((side, own), F32)
        for owner in range(n_row):
            mark = marked[owner, pl.ds(r, 1), :]
            piece = adjacency[rows, owner * own:(owner + 1) * own].astype(F32) * mark
            square = square + piece * piece
            masked[owner, rows, :] = piece.astype(BF16)
        squares[rows, :] = square

    if n_row * row_blocks <= 64:
        for r in range(row_blocks):
            mask_rows(r)
    else:
        pl.loop(0, row_blocks)(mask_rows)

    pl.semaphore_wait(barrier, n_hi + n_lo + n_col - 3)
    send_own(rows_in, 0)

    ones = jnp.ones((8, own), BF16)
    high = squares[...].astype(BF16)
    low = (squares[...] - high.astype(F32)).astype(BF16)
    contract = (((1,), (1,)), ((), ()))
    sums = lax.dot_general(ones, high, contract, preferred_element_type=F32)
    sums = sums + lax.dot_general(ones, low, contract, preferred_element_type=F32)
    for peer in range(n_col):
        degree_send[peer] = sums[:, peer * own:(peer + 1) * own]
    for step in range(1, n_col):
        degree_copy(step).start()
    degree = 1.0 + degree_send[col]
    for step in range(1, n_col):
        degree_copy(step).wait_recv()
        degree = degree + degree_got[step]
    roots[row] = lax.rsqrt(degree)
    for step in range(1, n_hi):
        root_hi(step, row).start()
    for step in range(1, n_lo):
        root_lo(0, step, row).start()

    def root_column(owner):
        return jnp.broadcast_to(roots[owner, 0:1, :], (own, own)).T

    inv_root = root_column(row)

    def layer(buffer, index):
        def add(half, owner, fresh=False):
            values = buffer[half, owner]
            if index == 0:
                values = (root_column(owner) * values.astype(F32)).astype(BF16)
            product = jnp.dot(masked[owner], values, preferred_element_type=F32)
            if fresh:
                total[half] = product
            else:
                total[half] += product

        for half in range(halves):
            add(half, row, True)
        for half in range(halves):
            pass_on(buffer, index, half)
            if index == 0 and half == 0:
                for back in range(1, n_hi):
                    root_hi(back, row).wait_recv()
                    for step in range(1, n_lo):
                        root_lo(back, step, holder(back)).start()
        for half in range(halves):
            for back in range(1, n_hi):
                add(half, holder(back))
            for back in range(n_hi):
                def arrived(step):
                    owner = lax.rem(hi + n_hi - back, n_hi) * n_lo + lax.rem(lo + n_lo - step, n_lo)
                    lo_copy(buffer, index, half, back, step, row).wait_recv()
                    if index == 0 and half == 0:
                        root_lo(back, step, row).wait_recv()
                    add(half, owner)

                if n_lo <= 4:
                    for step in range(1, n_lo):
                        arrived(step)
                else:
                    pl.loop(1, n_lo)(arrived)
            yield half

    def collect(buffer, source, landing, index):
        for half in layer(buffer, index):
            for step in range(1, n_col):
                rows = pl.ds(pl.multiple_of(col_peer(step) * own, own), own)
                source[half, step] = total[half, rows, :].astype(BF16)
                part_copy(source, landing, index, half, step).start()
        sums = []
        for half in range(halves):
            mine = total[half, pl.ds(pl.multiple_of(col * own, own), own), :]
            for step in range(1, n_col):
                part_copy(source, landing, index, half, step).wait_recv()
                mine = mine + landing[half, step].astype(F32)
            sums.append(mine)
        return sums

    def cut(value, half):
        return value[:, half * width:(half + 1) * width]

    loads[4].wait()
    loads[5].wait()
    loads[6].wait()
    summed = collect(rows_in, part_in, got_in, 0)
    projected_out = jnp.zeros((own, halves * width), F32)
    for half in range(halves):
        hidden = inv_root * (summed[half] + inv_root * cut(projected, half)) + cut(bias_in[...], half)
        hidden = jnp.maximum(hidden, 0.0).astype(BF16)
        projected_out += jnp.dot(
            hidden, weight_out[half * width:(half + 1) * width, :], preferred_element_type=F32
        )
    scaled_out = [inv_root * cut(projected_out, half) for half in range(halves)]
    for half in range(halves):
        rows_out[half, row] = scaled_out[half].astype(BF16)
    send_own(rows_out, 1)
    summed_out = collect(rows_out, part_out, got_out, 1)
    for half in range(halves):
        final = inv_root * (summed_out[half] + scaled_out[half]) + cut(bias_out[...], half)
        out[:, half * width:(half + 1) * width] = final.astype(BF16)

    for layer_index, (buffer, source, landing) in enumerate(
        ((rows_in, part_in, got_in), (rows_out, part_out, got_out))
    ):
        for half in range(halves):
            for step in range(1, n_hi):
                hi_copy(buffer, layer_index, half, step, row).wait_send()
            for back in range(n_hi):
                for step in range(1, n_lo):
                    lo_copy(buffer, layer_index, half, back, step, row).wait_send()
            for step in range(1, n_col):
                part_copy(source, landing, layer_index, half, step).wait_send()
    for step in range(1, n_col):
        degree_copy(step).wait_send()
    for back in range(1, n_hi):
        root_hi(back, row).wait_send()
    for back in range(n_hi):
        for step in range(1, n_lo):
            root_lo(back, step, row).wait_send()


def body(n_row, n_lo, n_col, features, adjacency, pattern, weight_in, bias_in, weight_out, bias_out):
    own, width = features.shape[0], weight_out.shape[1]
    height = adjacency.shape[0]
    half = own
    halves = width // half
    n_hi = n_row // n_lo
    dma = pltpu.SemaphoreType.DMA
    args = (features, adjacency, pattern, weight_in, bias_in[None, :], weight_out, bias_out[None, :])
    return pl.pallas_call(
        functools.partial(kernel, n_lo, n_col),
        out_shape=jax.ShapeDtypeStruct((own, width), BF16),
        in_specs=[pl.BlockSpec(memory_space=pl.ANY)] * len(args),
        out_specs=pl.BlockSpec(memory_space=pltpu.VMEM),
        scratch_shapes=[pltpu.VMEM(arg.shape, arg.dtype) for arg in args] + [
            pltpu.VMEM((n_row, height, own), BF16),
            pltpu.VMEM((height, own), F32),
            pltpu.VMEM((n_row, pattern.shape[0], own), F32),
            pltpu.VMEM((halves, height, half), F32),
            pltpu.VMEM((halves, n_row, own, half), BF16),
            pltpu.VMEM((halves, n_row, own, half), BF16),
            pltpu.VMEM((halves, n_col, own, half), BF16),
            pltpu.VMEM((halves, n_col, own, half), BF16),
            pltpu.VMEM((halves, n_col, own, half), BF16),
            pltpu.VMEM((halves, n_col, own, half), BF16),
            pltpu.VMEM((n_col, 8, own), F32),
            pltpu.VMEM((n_col, 8, own), F32),
            pltpu.VMEM((n_row, 8, own), F32),
            dma((len(args),)),
            dma((2, halves, n_hi)), dma((2, halves, n_hi)),
            dma((2, halves, n_hi, n_lo)), dma((2, halves, n_hi, n_lo)),
            dma((2, halves, n_col)), dma((2, halves, n_col)),
            dma((n_col,)), dma((n_col,)), dma((n_hi, n_lo)), dma((n_hi, n_lo)),
        ],
        compiler_params=pltpu.CompilerParams(
            collective_id=0, has_side_effects=True, vmem_limit_bytes=60 * 1024 * 1024
        ),
    )(*args)


def fast_extent(mesh):
    count = mesh.shape["row"]
    places = [tuple(getattr(device, "coords", None) or ()) for device in mesh.devices[:, 0]]
    if not places[0]:
        return 2 if count % 2 == 0 else 1
    moved = [[a != b for a, b in zip(place, places[0])] for place in places]
    extent = 2
    while extent < count and moved[extent] == moved[1]:
        extent += 1
    return extent


def solution(mesh):
    placed = (P(("row", "col"), None), P("row", "col"), P("row", "col"), P(), P(), P(), P())
    return jax.shard_map(
        functools.partial(body, mesh.shape["row"], fast_extent(mesh), mesh.shape["col"]),
        mesh=mesh, in_specs=placed, out_specs=P(("row", "col"), None), check_vma=False,
    )
```

time: 136 us -> 37.4 us (0.27)
  blocking collectives: 71.7 us -> 0 us
  waiting for transfers between devices: 40.4 us -> 0 us
  Pallas kernels: 0 us -> 35.8 us
  between operations: 14.1 us -> 0.01 us
  matrix products: 3.52 us -> 0 us
  other arithmetic: 2.85 us -> 0 us
  local copies, waits for them, and re-layouts: 3.35 us -> 1.47 us
    all_gather x2 -> x0, blocking collectives: 63.4 us -> none  [the longest x1 31.9 us: body(): gathered = lax.all_gather(own_rows, 'row', axis=0, tiled=True)]
    reduce_scatter x2 -> x0, waiting for transfers between devices: 40.4 us -> none  [collect(): lax.psum_scatter(partial_value.astype(jnp.bfloat16), 'col', scatter_dimen...]
    pallas_call x0 -> x1, Pallas kernels: none -> 35.8 us  [body(): pl.pallas_call(functools.partial(kernel, n_lo, n_col), out_shape=jax.Shap...]
    unnamed x1 -> x0, blocking collectives: 8.4 us -> none
    dot_general x4 -> x0, matrix products: 3.52 us -> none  [the longest x2 2.28 us: product(): return jnp.dot(masked, gathered, preferred_element_type=jnp.float32)]
    broadcast_in_dim x2 -> x0, local copies, waits for them, and re-layouts: 2.73 us -> none  [body(): jnp.where(present, adjacency.reshape(row_blocks, BLK, col_blocks, BLK), j...]
    convert_element_type x1 -> x0, other arithmetic: 1.56 us -> none  [body(): return (inv_root * summed_out + bias_out[None, :]).astype(jnp.bfloat16)]
  transfers between devices with their start and end apart: 2 -> 0, of which waited for: 2 -> 0; matrix products, arithmetic and copies ran while one was open for 0% -> 0% of each run, Pallas kernels for 0% -> 0%
where the time goes in v2:
time: 37.4 us; the launch traced here: 37.2 us
  Pallas kernels  35.8 us (96%)
  local copies, waits for them, and re-layouts  1.47 us (4%)
    pallas_call x1, Pallas kernels, body(): pl.pallas_call(functools.partial(kernel, n_lo, n_col), out_shape=jax.Shap...  35.8 us
    unnamed x1, local copies, waits for them, and re-layouts  1.47 us

profile of v2, /device:TPU:0, one launch (start us, length us, event | category | flops | bytes accessed | tf_op | source)
XLA Modules:
  0.0 37.2 jit_solution(4408380424375317897)
XLA Ops:
  0.0 35.8 %shard_map.73 = bf16[128,256]{1,0:T(8,128)(2,1)} custom-call(bf16[128,512]{1,0:T(8,128)(2,1)} %features_in.1, bf16[512,1024]{1,0:T(8,128)(2,1)} %adjacency_in.1, s32[8,16]{1,0:T(8,128)} %pattern_in.1, bf16[512,256]{1,0:T(8,128)(2,1)} %weight_one_in.1, f32[1,256]{1,0:T(1,128)} %bitcast.2, bf16[256,256]{1,0:T(8,128)(2,1)} %weight_two_in.1, f32[1,256]{1,0:T(1,128)} %bitcast.3), custom_call_target="tpu_custom_call" | custom-call | tf_op jit(solution)/shard_map/pallas_call | solution.py:284
  35.8 1.5 %copy.9 = bf16[128,256]{1,0:T(8,128)(2,1)} copy(bf16[128,256]{1,0:T(8,128)(2,1)} %shard_map.73) | data formatting | bytes 131072
